TPU v7x, 32 devices: a whole 2x2x4 slice. The times are simulated.
32 devices in a mesh: lat: 4 (over z), lon: 4 (over x, core), lev: 2 (over y).
Axes of the slice: x: 2, y: 2, z: 4, core: 2. Of those that a mesh axis runs over, the one named last changes fastest.
Arguments:
- field_now: float32 [16, 256, 128, 128], P('lat', 'lon', 'lev'), may hold values from 0.2 to 1.8
- earlier: float32 [16, 256, 128, 128], P('lat', 'lon', 'lev'), may hold values from 0.2 to 1.8
- speed_square: float32 [16, 256, 128, 128], P('lat', 'lon', 'lev'), may hold values from 0.05 to 0.3
Outputs:
- field_now_end: float32 [16, 256, 128, 128], P('lat', 'lon', 'lev')
All inputs are finite; a program needn't handle non-finite values.
Results may differ from a plain program's by a relative error of at most 0.00002.
Values sent between devices are 32-bit elements; how exact they have to be, the bound alone decides.
A program may use at most 320 MiB of HBM per device.

v0:
```python
import jax
import jax.numpy as jnp
from jax import lax
from jax.sharding import PartitionSpec as P

STEPS = 4


def extended(value, sides, width):
    for axis, dim in sides:
        peers, length = (lax.axis_size(axis), value.shape[dim])
        up = [(i, (i + 1) % peers) for i in range(peers - 1)]
        down = [(j, i) for i, j in up]
        last = lax.slice_in_dim(value, length - width, length, axis=dim)
        initial = lax.slice_in_dim(value, 0, width, axis=dim)
        before = lax.ppermute(last, axis, up)
        after = lax.ppermute(initial, axis, down)
        value = jnp.concatenate([before, value, after], axis=dim)
    return value


def without_rim(values, dims):
    for dim in dims:
        values = lax.slice_in_dim(values, 1, values.shape[dim] - 1, axis=dim)
    return values


def shifted_cells(values, dim, start, dims):
    others = [other for other in dims if other != dim]
    values = without_rim(values, others)
    return lax.slice_in_dim(values, start, start + values.shape[dim] - 2, axis=dim)


def march_step(padded, before, speed_square):
    middle = without_rim(padded, (0, 1, 2))
    lower = [shifted_cells(padded, dim, 0, (0, 1, 2)) for dim in (0, 1, 2)]
    upper = [shifted_cells(padded, dim, 2, (0, 1, 2)) for dim in (0, 1, 2)]
    spread = lower[0] + upper[0] + lower[1] + upper[1] + lower[2] + upper[2] - 6.0 * middle
    return 2.0 * middle - before + speed_square * spread


def local(field_now, earlier, speed_square):
    for step in range(STEPS):
        padded = extended(field_now, (("lat", 0), ("lon", 1), ("lev", 2)), 1)
        later = march_step(padded, earlier, speed_square)
        earlier, field_now = (field_now, later)
    return field_now


def solution(mesh):
    return jax.shard_map(
        local,
        mesh=mesh,
        in_specs=(
            P("lat", "lon", "lev", None),
            P("lat", "lon", "lev", None),
            P("lat", "lon", "lev", None),
        ),
        out_specs=P("lat", "lon", "lev", None),
        check_vma=False,
    )
```

profile of v0, /device:TPU:0, one launch (start us, length us, event | category | flops | bytes accessed | tf_op | source)
XLA Modules:
  0.0 403.9 jit_solution(15187204011936680499)
XLA Ops:
  0.0 4.1 %fusion.36 = (f32[1,64,64,128]{3,2,1,0:T(8,128)}, f32[1,64,64,128]{3,2,1,0:T(8,128)S(1)}) fusion(f32[4,64,64,128]{3,2,1,0:T(8,128)} %param.3), kind=kLoop, calls=%fused_computation.130 | loop fusion | bytes 8388608 | tf_op jit(solution)/shard_map/slice | solution.py:15
  4.1 5.2 %collective-permute-start = (f32[1,64,64,128]{3,2,1,0:T(8,128)S(1)}, f32[1,64,64,128]{3,2,1,0:T(8,128)S(1)}, u32[]{:S(2)}, u32[]{:S(2)}) collective-permute-start(f32[1,64,64,128]{3,2,1,0:T(8,128)S(1)} %get-tuple-element.28), channel_id=1, source_target_pairs={{0,8},{8,16},{16,24},{1,9},{9,17},{17,25},{2,10},{10,18},{18,26},{... | collective-permute-start | bytes 6291464 | tf_op jit(solution)/shard_map/ppermute | solution.py:16
  9.4 1.3 collective-permute-start.1
  10.7 43.4 %collective-permute-done = f32[1,64,64,128]{3,2,1,0:T(8,128)S(1)} collective-permute-done((f32[1,64,64,128]{3,2,1,0:T(8,128)S(1)}, f32[1,64,64,128]{3,2,1,0:T(8,128)S(1)}, u32[]{:S(2)}, u32[]{:S(2)}) %collective-permute-start) | collective-permute-done | bytes 2097184 | tf_op jit(solution)/shard_map/ppermute | solution.py:16
  55.6 1.7 constant_dynamic-update-slice_fusion.1
  57.3 1.4 collective-permute-done.1
  58.7 1.7 constant_dynamic-update-slice_fusion
  60.4 1.3 collective-permute-start.2
  61.8 1.3 collective-permute-start.3
  63.1 3.7 collective-permute-done.3
  67.1 1.3 collective-permute-start.5
  68.4 4.6 %collective-permute-start.4 = (f32[6,66,1,128]{3,1,2,0:T(8,128)S(1)}, f32[6,66,1,128]{3,1,2,0:T(8,128)S(1)}, u32[]{:S(2)}, u32[]{:S(2)}) collective-permute-start(f32[6,66,1,128]{3,1,2,0:T(8,128)S(1)} %copy.18), channel_id=1, source_target_pairs={{0,1},{2,3},{4,5},{6,7},{8,9},{10,11},{12,13},{14,15},{16,17},{18,... | collective-permute-start | bytes 608264 | tf_op jit(solution)/shard_map/ppermute | solution.py:16
  73.0 1.9 collective-permute-done.5
  76.6 27.5 %fusion.27 = f32[4,64,64,128]{3,2,1,0:T(8,128)S(1)} fusion(f32[4,64,64,128]{3,2,1,0:T(8,128)} %param.5, f32[6,66,1,128]{3,2,1,0:T(1,128)S(1)} %copy.21, f32[6,1,64,128]{3,2,1,0:T(8,128)S(1)} %collective-permute-done.3, f32[6,64,64,128]{3,2,1,0:T(8,128)} %copy-done.4, f32[6,1,64,128]{3,2,1,0:T(8,128)S(1)} %collective-permute-done.2, ...), kind=kLoop, calls=%fused_computation.82 | loop fusion | flops 44040192 | bytes 51130368 | tf_op jit(solution)/shard_map/add | solution.py:39
  104.7 3.5 collective-permute-start.6
  108.2 1.3 collective-permute-start.7
  109.5 42.5 %collective-permute-done.6 = f32[1,64,64,128]{3,2,1,0:T(8,128)S(1)} collective-permute-done((f32[1,64,64,128]{3,2,1,0:T(8,128)S(1)}, f32[1,64,64,128]{3,2,1,0:T(8,128)S(1)}, u32[]{:S(2)}, u32[]{:S(2)}) %collective-permute-start.6) | collective-permute-done | bytes 2097184 | tf_op jit(solution)/shard_map/ppermute | solution.py:16
  152.1 4.8 %collective-permute-done.7 = f32[1,64,64,128]{3,2,1,0:T(8,128)S(1)} collective-permute-done((f32[1,64,64,128]{3,2,1,0:T(8,128)S(1)}, f32[1,64,64,128]{3,2,1,0:T(8,128)S(1)}, u32[]{:S(2)}, u32[]{:S(2)}) %collective-permute-start.7) | collective-permute-done | bytes 2097184 | tf_op jit(solution)/shard_map/ppermute | solution.py:17
  156.9 3.5 collective-permute-start.8
  160.4 1.3 collective-permute-start.9
  161.7 2.0 collective-permute-done.9
  164.1 1.3 collective-permute-start.11
  165.4 4.7 %collective-permute-start.10 = (f32[6,66,1,128]{3,1,2,0:T(8,128)S(1)}, f32[6,66,1,128]{3,1,2,0:T(8,128)S(1)}, u32[]{:S(2)}, u32[]{:S(2)}) collective-permute-start(f32[6,66,1,128]{3,1,2,0:T(8,128)S(1)} %copy.22), channel_id=1, source_target_pairs={{0,1},{2,3},{4,5},{6,7},{8,9},{10,11},{12,13},{14,15},{16,17},{18,... | collective-permute-start | bytes 608264 | tf_op jit(solution)/shard_map/ppermute | solution.py:16
  170.1 1.7 collective-permute-done.11
  173.6 28.9 %fusion.19 = f32[4,64,64,128]{3,2,1,0:T(8,128)} fusion(f32[4,64,64,128]{3,2,1,0:T(8,128)} %param.5, f32[6,66,1,128]{3,2,1,0:T(1,128)S(1)} %copy.25, f32[6,1,64,128]{3,2,1,0:T(8,128)S(1)} %collective-permute-done.9, f32[6,1,64,128]{3,2,1,0:T(8,128)S(1)} %collective-permute-done.8, f32[1,64,64,128]{3,2,1,0:T(8,128)} %copy-done.7, ...), kind=kLoop, calls=%fused_computation.56 | loop fusion | flops 60817408 | bytes 38547456 | tf_op jit(solution)/shard_map/add | solution.py:39
  202.5 2.7 fusion.34
  205.2 3.7 collective-permute-start.12
  209.0 1.3 collective-permute-start.13
  210.3 42.9 %collective-permute-done.12 = f32[1,64,64,128]{3,2,1,0:T(8,128)S(1)} collective-permute-done((f32[1,64,64,128]{3,2,1,0:T(8,128)S(1)}, f32[1,64,64,128]{3,2,1,0:T(8,128)S(1)}, u32[]{:S(2)}, u32[]{:S(2)}) %collective-permute-start.12) | collective-permute-done | bytes 2097184 | tf_op jit(solution)/shard_map/ppermute | solution.py:16
  253.2 4.8 %collective-permute-done.13 = f32[1,64,64,128]{3,2,1,0:T(8,128)S(1)} collective-permute-done((f32[1,64,64,128]{3,2,1,0:T(8,128)S(1)}, f32[1,64,64,128]{3,2,1,0:T(8,128)S(1)}, u32[]{:S(2)}, u32[]{:S(2)}) %collective-permute-start.13) | collective-permute-done | bytes 2097184 | tf_op jit(solution)/shard_map/ppermute | solution.py:17
  258.0 3.1 collective-permute-start.14
  261.2 1.3 collective-permute-start.15
  262.5 2.0 collective-permute-done.15
  264.8 1.3 collective-permute-start.17
  266.1 4.6 %collective-permute-start.16 = (f32[6,66,1,128]{3,1,2,0:T(8,128)S(1)}, f32[6,66,1,128]{3,1,2,0:T(8,128)S(1)}, u32[]{:S(2)}, u32[]{:S(2)}) collective-permute-start(f32[6,66,1,128]{3,1,2,0:T(8,128)S(1)} %copy.26), channel_id=1, source_target_pairs={{0,1},{2,3},{4,5},{6,7},{8,9},{10,11},{12,13},{14,15},{16,17},{18,... | collective-permute-start | bytes 608264 | tf_op jit(solution)/shard_map/ppermute | solution.py:16
  270.7 1.9 collective-permute-done.17
  274.4 28.9 %fusion.11 = f32[4,64,64,128]{3,2,1,0:T(8,128)} fusion(f32[4,64,64,128]{3,2,1,0:T(8,128)} %param.5, f32[6,66,1,128]{3,2,1,0:T(1,128)S(1)} %copy.29, f32[6,1,64,128]{3,2,1,0:T(8,128)S(1)} %collective-permute-done.15, f32[6,1,64,128]{3,2,1,0:T(8,128)S(1)} %collective-permute-done.14, f32[1,64,64,128]{3,2,1,0:T(8,128)} %copy-done.6, ...), kind=kLoop, calls=%fused_computation.30 | loop fusion | flops 60817408 | bytes 38547456 | tf_op jit(solution)/shard_map/add | solution.py:39
  303.3 2.7 fusion.33
  306.0 3.4 collective-permute-start.18
  309.5 1.3 collective-permute-start.19
  310.8 42.9 %collective-permute-done.18 = f32[1,64,64,128]{3,2,1,0:T(8,128)S(1)} collective-permute-done((f32[1,64,64,128]{3,2,1,0:T(8,128)S(1)}, f32[1,64,64,128]{3,2,1,0:T(8,128)S(1)}, u32[]{:S(2)}, u32[]{:S(2)}) %collective-permute-start.18) | collective-permute-done | bytes 2097184 | tf_op jit(solution)/shard_map/ppermute | solution.py:16
  353.6 4.8 %collective-permute-done.19 = f32[1,64,64,128]{3,2,1,0:T(8,128)S(1)} collective-permute-done((f32[1,64,64,128]{3,2,1,0:T(8,128)S(1)}, f32[1,64,64,128]{3,2,1,0:T(8,128)S(1)}, u32[]{:S(2)}, u32[]{:S(2)}) %collective-permute-start.19) | collective-permute-done | bytes 2097184 | tf_op jit(solution)/shard_map/ppermute | solution.py:17
  358.5 3.1 collective-permute-start.20
  362.9 2.0 collective-permute-done.21
  365.3 1.3 collective-permute-start.23
  366.6 4.8 %collective-permute-start.22 = (f32[6,66,1,128]{3,1,2,0:T(8,128)S(1)}, f32[6,66,1,128]{3,1,2,0:T(8,128)S(1)}, u32[]{:S(2)}, u32[]{:S(2)}) collective-permute-start(f32[6,66,1,128]{3,1,2,0:T(8,128)S(1)} %copy.30), channel_id=1, source_target_pairs={{0,1},{2,3},{4,5},{6,7},{8,9},{10,11},{12,13},{14,15},{16,17},{18,... | collective-permute-start | bytes 608264 | tf_op jit(solution)/shard_map/ppermute | solution.py:16
  371.4 1.7 collective-permute-done.23
  374.8 28.9 %fusion.3 = f32[4,64,64,128]{3,2,1,0:T(8,128)} fusion(f32[4,64,64,128]{3,2,1,0:T(8,128)} %param.5, f32[6,66,1,128]{3,2,1,0:T(1,128)S(1)} %copy.33, f32[6,1,64,128]{3,2,1,0:T(8,128)S(1)} %collective-permute-done.21, f32[6,1,64,128]{3,2,1,0:T(8,128)S(1)} %collective-permute-done.20, f32[1,64,64,128]{3,2,1,0:T(8,128)} %copy-done.5, ...), kind=kLoop, calls=%fused_computation.4 | loop fusion | flops 60817408 | bytes 38547456 | tf_op jit(solution)/shard_map/add | solution.py:39
  (53 shorter events, 11.5 us)
Async XLA Ops:
  0.0 55.6 %copy-start.3 = (f32[4,64,64,128]{3,2,1,0:T(8,128)S(1)}, f32[4,64,64,128]{3,2,1,0:T(8,128)}, u32[]{:S(2)}) copy-start(f32[4,64,64,128]{3,2,1,0:T(8,128)} %param.3) | copy-start | bytes 25165828
  4.1 50.0 %collective-permute-start = (f32[1,64,64,128]{3,2,1,0:T(8,128)S(1)}, f32[1,64,64,128]{3,2,1,0:T(8,128)S(1)}, u32[]{:S(2)}, u32[]{:S(2)}) collective-permute-start(f32[1,64,64,128]{3,2,1,0:T(8,128)S(1)} %get-tuple-element.28), channel_id=1, source_target_pairs={{0,8},{8,16},{16,24},{1,9},{9,17},{17,25},{2,10},{10,18},{18,26},{... | collective-permute-start | bytes 6291464 | tf_op jit(solution)/shard_map/ppermute | solution.py:16
  9.4 49.3 %collective-permute-start.1 = (f32[1,64,64,128]{3,2,1,0:T(8,128)}, f32[1,64,64,128]{3,2,1,0:T(8,128)}, u32[]{:S(2)}, u32[]{:S(2)}) collective-permute-start(f32[1,64,64,128]{3,2,1,0:T(8,128)} %get-tuple-element.27), channel_id=1, source_target_pairs={{8,0},{16,8},{24,16},{9,1},{17,9},{25,17},{10,2},{18,10},{26,18},{... | collective-permute-start | bytes 6291464 | tf_op jit(solution)/shard_map/ppermute | solution.py:17
  54.1 1.3 copy-start.8
  60.4 16.0 %copy-start.4 = (f32[6,64,64,128]{3,2,1,0:T(8,128)}, f32[6,64,64,128]{3,2,1,0:T(8,128)S(1)}, u32[]{:S(2)}) copy-start(f32[6,64,64,128]{3,2,1,0:T(8,128)S(1)} %constant_dynamic-update-slice_fusion) | copy-start | bytes 37748740
  60.4 2.6 collective-permute-start.2
  61.8 5.1 %collective-permute-start.3 = (f32[6,1,64,128]{3,2,1,0:T(8,128)S(1)}, f32[6,1,64,128]{3,2,1,0:T(8,128)S(1)}, u32[]{:S(2)}, u32[]{:S(2)}) collective-permute-start(f32[6,1,64,128]{3,2,1,0:T(8,128)S(1)} %get-tuple-element.20), channel_id=1, source_target_pairs={{2,0},{4,2},{6,4},{3,1},{5,3},{7,5},{10,8},{12,10},{14,12},{11,9},... | collective-permute-start | bytes 589832 | tf_op jit(solution)/shard_map/ppermute | solution.py:17
  67.1 7.8 %collective-permute-start.5 = (f32[6,66,1,128]{3,1,2,0:T(8,128)S(1)}, f32[6,66,1,128]{3,1,2,0:T(8,128)S(1)}, u32[]{:S(2)}, u32[]{:S(2)}) collective-permute-start(f32[6,66,1,128]{3,1,2,0:T(8,128)S(1)} %copy.20), channel_id=1, source_target_pairs={{1,0},{3,2},{5,4},{7,6},{9,8},{11,10},{13,12},{15,14},{17,16},{19,... | collective-permute-start | bytes 608264 | tf_op jit(solution)/shard_map/ppermute | solution.py:17
  68.4 8.0 %collective-permute-start.4 = (f32[6,66,1,128]{3,1,2,0:T(8,128)S(1)}, f32[6,66,1,128]{3,1,2,0:T(8,128)S(1)}, u32[]{:S(2)}, u32[]{:S(2)}) collective-permute-start(f32[6,66,1,128]{3,1,2,0:T(8,128)S(1)} %copy.18), channel_id=1, source_target_pairs={{0,1},{2,3},{4,5},{6,7},{8,9},{10,11},{12,13},{14,15},{16,17},{18,... | collective-permute-start | bytes 608264 | tf_op jit(solution)/shard_map/ppermute | solution.py:16
  104.2 59.6 %copy-start = (f32[4,64,64,128]{3,2,1,0:T(8,128)}, f32[4,64,64,128]{3,2,1,0:T(8,128)S(1)}, u32[]{:S(2)}) copy-start(f32[4,64,64,128]{3,2,1,0:T(8,128)S(1)} %fusion.27) | copy-start | bytes 25165828
  104.7 47.3 %collective-permute-start.6 = (f32[1,64,64,128]{3,2,1,0:T(8,128)S(1)}, f32[1,64,64,128]{3,2,1,0:T(8,128)S(1)}, u32[]{:S(2)}, u32[]{:S(2)}) collective-permute-start(f32[1,64,64,128]{3,2,1,0:T(8,128)S(1)} %get-tuple-element.25), channel_id=1, source_target_pairs={{0,8},{8,16},{16,24},{1,9},{9,17},{17,25},{2,10},{10,18},{18,26},{... | collective-permute-start | bytes 6291464 | tf_op jit(solution)/shard_map/ppermute | solution.py:16
  108.2 48.6 %collective-permute-start.7 = (f32[1,64,64,128]{3,2,1,0:T(8,128)S(1)}, f32[1,64,64,128]{3,2,1,0:T(8,128)S(1)}, u32[]{:S(2)}, u32[]{:S(2)}) collective-permute-start(f32[1,64,64,128]{3,2,1,0:T(8,128)S(1)} %get-tuple-element.26), channel_id=1, source_target_pairs={{8,0},{16,8},{24,16},{9,1},{17,9},{25,17},{10,2},{18,10},{26,18},{... | collective-permute-start | bytes 6291464 | tf_op jit(solution)/shard_map/ppermute | solution.py:17
  156.9 7.2 %copy-start.7 = (f32[1,64,64,128]{3,2,1,0:T(8,128)}, f32[1,64,64,128]{3,2,1,0:T(8,128)S(1)}, u32[]{:S(2)}) copy-start(f32[1,64,64,128]{3,2,1,0:T(8,128)S(1)} %collective-permute-done.7) | copy-start | bytes 6291460
  156.9 4.8 %collective-permute-start.8 = (f32[6,1,64,128]{3,2,1,0:T(8,128)S(1)}, f32[6,1,64,128]{3,2,1,0:T(8,128)S(1)}, u32[]{:S(2)}, u32[]{:S(2)}) collective-permute-start(f32[6,1,64,128]{3,2,1,0:T(8,128)S(1)} %get-tuple-element.17), channel_id=1, source_target_pairs={{0,2},{2,4},{4,6},{1,3},{3,5},{5,7},{8,10},{10,12},{12,14},{9,11},... | collective-permute-start | bytes 589832 | tf_op jit(solution)/shard_map/ppermute | solution.py:16
  160.4 3.3 collective-permute-start.9
  164.1 7.8 %collective-permute-start.11 = (f32[6,66,1,128]{3,1,2,0:T(8,128)S(1)}, f32[6,66,1,128]{3,1,2,0:T(8,128)S(1)}, u32[]{:S(2)}, u32[]{:S(2)}) collective-permute-start(f32[6,66,1,128]{3,1,2,0:T(8,128)S(1)} %copy.24), channel_id=1, source_target_pairs={{1,0},{3,2},{5,4},{7,6},{9,8},{11,10},{13,12},{15,14},{17,16},{19,... | collective-permute-start | bytes 608264 | tf_op jit(solution)/shard_map/ppermute | solution.py:17
  165.4 8.0 %collective-permute-start.10 = (f32[6,66,1,128]{3,1,2,0:T(8,128)S(1)}, f32[6,66,1,128]{3,1,2,0:T(8,128)S(1)}, u32[]{:S(2)}, u32[]{:S(2)}) collective-permute-start(f32[6,66,1,128]{3,1,2,0:T(8,128)S(1)} %copy.22), channel_id=1, source_target_pairs={{0,1},{2,3},{4,5},{6,7},{8,9},{10,11},{12,13},{14,15},{16,17},{18,... | collective-permute-start | bytes 608264 | tf_op jit(solution)/shard_map/ppermute | solution.py:16
  202.5 55.5 %copy-start.1 = (f32[4,64,64,128]{3,2,1,0:T(8,128)S(1)}, f32[4,64,64,128]{3,2,1,0:T(8,128)}, u32[]{:S(2)}) copy-start(f32[4,64,64,128]{3,2,1,0:T(8,128)} %fusion.19) | copy-start | bytes 25165828
  205.2 47.9 %collective-permute-start.12 = (f32[1,64,64,128]{3,2,1,0:T(8,128)S(1)}, f32[1,64,64,128]{3,2,1,0:T(8,128)S(1)}, u32[]{:S(2)}, u32[]{:S(2)}) collective-permute-start(f32[1,64,64,128]{3,2,1,0:T(8,128)S(1)} %get-tuple-element.23), channel_id=1, source_target_pairs={{0,8},{8,16},{16,24},{1,9},{9,17},{17,25},{2,10},{10,18},{18,26},{... | collective-permute-start | bytes 6291464 | tf_op jit(solution)/shard_map/ppermute | solution.py:16
  209.0 49.0 %collective-permute-start.13 = (f32[1,64,64,128]{3,2,1,0:T(8,128)S(1)}, f32[1,64,64,128]{3,2,1,0:T(8,128)S(1)}, u32[]{:S(2)}, u32[]{:S(2)}) collective-permute-start(f32[1,64,64,128]{3,2,1,0:T(8,128)S(1)} %get-tuple-element.24), channel_id=1, source_target_pairs={{8,0},{16,8},{24,16},{9,1},{17,9},{25,17},{10,2},{18,10},{26,18},{... | collective-permute-start | bytes 6291464 | tf_op jit(solution)/shard_map/ppermute | solution.py:17
  258.0 6.8 %copy-start.6 = (f32[1,64,64,128]{3,2,1,0:T(8,128)}, f32[1,64,64,128]{3,2,1,0:T(8,128)S(1)}, u32[]{:S(2)}) copy-start(f32[1,64,64,128]{3,2,1,0:T(8,128)S(1)} %collective-permute-done.13) | copy-start | bytes 6291460
  258.0 4.4 %collective-permute-start.14 = (f32[6,1,64,128]{3,2,1,0:T(8,128)S(1)}, f32[6,1,64,128]{3,2,1,0:T(8,128)S(1)}, u32[]{:S(2)}, u32[]{:S(2)}) collective-permute-start(f32[6,1,64,128]{3,2,1,0:T(8,128)S(1)} %get-tuple-element.15), channel_id=1, source_target_pairs={{0,2},{2,4},{4,6},{1,3},{3,5},{5,7},{8,10},{10,12},{12,14},{9,11},... | collective-permute-start | bytes 589832 | tf_op jit(solution)/shard_map/ppermute | solution.py:16
  261.2 3.3 collective-permute-start.15
  264.8 7.8 %collective-permute-start.17 = (f32[6,66,1,128]{3,1,2,0:T(8,128)S(1)}, f32[6,66,1,128]{3,1,2,0:T(8,128)S(1)}, u32[]{:S(2)}, u32[]{:S(2)}) collective-permute-start(f32[6,66,1,128]{3,1,2,0:T(8,128)S(1)} %copy.28), channel_id=1, source_target_pairs={{1,0},{3,2},{5,4},{7,6},{9,8},{11,10},{13,12},{15,14},{17,16},{19,... | collective-permute-start | bytes 608264 | tf_op jit(solution)/shard_map/ppermute | solution.py:17
  266.1 8.0 %collective-permute-start.16 = (f32[6,66,1,128]{3,1,2,0:T(8,128)S(1)}, f32[6,66,1,128]{3,1,2,0:T(8,128)S(1)}, u32[]{:S(2)}, u32[]{:S(2)}) collective-permute-start(f32[6,66,1,128]{3,1,2,0:T(8,128)S(1)} %copy.26), channel_id=1, source_target_pairs={{0,1},{2,3},{4,5},{6,7},{8,9},{10,11},{12,13},{14,15},{16,17},{18,... | collective-permute-start | bytes 608264 | tf_op jit(solution)/shard_map/ppermute | solution.py:16
  303.3 55.2 %copy-start.2 = (f32[4,64,64,128]{3,2,1,0:T(8,128)S(1)}, f32[4,64,64,128]{3,2,1,0:T(8,128)}, u32[]{:S(2)}) copy-start(f32[4,64,64,128]{3,2,1,0:T(8,128)} %fusion.11) | copy-start | bytes 25165828
  306.0 47.6 %collective-permute-start.18 = (f32[1,64,64,128]{3,2,1,0:T(8,128)S(1)}, f32[1,64,64,128]{3,2,1,0:T(8,128)S(1)}, u32[]{:S(2)}, u32[]{:S(2)}) collective-permute-start(f32[1,64,64,128]{3,2,1,0:T(8,128)S(1)} %get-tuple-element.21), channel_id=1, source_target_pairs={{0,8},{8,16},{16,24},{1,9},{9,17},{17,25},{2,10},{10,18},{18,26},{... | collective-permute-start | bytes 6291464 | tf_op jit(solution)/shard_map/ppermute | solution.py:16
  309.5 49.0 %collective-permute-start.19 = (f32[1,64,64,128]{3,2,1,0:T(8,128)S(1)}, f32[1,64,64,128]{3,2,1,0:T(8,128)S(1)}, u32[]{:S(2)}, u32[]{:S(2)}) collective-permute-start(f32[1,64,64,128]{3,2,1,0:T(8,128)S(1)} %get-tuple-element.22), channel_id=1, source_target_pairs={{8,0},{16,8},{24,16},{9,1},{17,9},{25,17},{10,2},{18,10},{26,18},{... | collective-permute-start | bytes 6291464 | tf_op jit(solution)/shard_map/ppermute | solution.py:17
  358.5 6.8 %copy-start.5 = (f32[1,64,64,128]{3,2,1,0:T(8,128)}, f32[1,64,64,128]{3,2,1,0:T(8,128)S(1)}, u32[]{:S(2)}) copy-start(f32[1,64,64,128]{3,2,1,0:T(8,128)S(1)} %collective-permute-done.19) | copy-start | bytes 6291460
  358.5 4.4 %collective-permute-start.20 = (f32[6,1,64,128]{3,2,1,0:T(8,128)S(1)}, f32[6,1,64,128]{3,2,1,0:T(8,128)S(1)}, u32[]{:S(2)}, u32[]{:S(2)}) collective-permute-start(f32[6,1,64,128]{3,2,1,0:T(8,128)S(1)} %get-tuple-element.13), channel_id=1, source_target_pairs={{0,2},{2,4},{4,6},{1,3},{3,5},{5,7},{8,10},{10,12},{12,14},{9,11},... | collective-permute-start | bytes 589832 | tf_op jit(solution)/shard_map/ppermute | solution.py:16
  361.6 3.3 collective-permute-start.21
  365.3 7.8 %collective-permute-start.23 = (f32[6,66,1,128]{3,1,2,0:T(8,128)S(1)}, f32[6,66,1,128]{3,1,2,0:T(8,128)S(1)}, u32[]{:S(2)}, u32[]{:S(2)}) collective-permute-start(f32[6,66,1,128]{3,1,2,0:T(8,128)S(1)} %copy.32), channel_id=1, source_target_pairs={{1,0},{3,2},{5,4},{7,6},{9,8},{11,10},{13,12},{15,14},{17,16},{19,... | collective-permute-start | bytes 608264 | tf_op jit(solution)/shard_map/ppermute | solution.py:17
  366.6 8.0 %collective-permute-start.22 = (f32[6,66,1,128]{3,1,2,0:T(8,128)S(1)}, f32[6,66,1,128]{3,1,2,0:T(8,128)S(1)}, u32[]{:S(2)}, u32[]{:S(2)}) collective-permute-start(f32[6,66,1,128]{3,1,2,0:T(8,128)S(1)} %copy.30), channel_id=1, source_target_pairs={{0,1},{2,3},{4,5},{6,7},{8,9},{10,11},{12,13},{14,15},{16,17},{18,... | collective-permute-start | bytes 608264 | tf_op jit(solution)/shard_map/ppermute | solution.py:16
where the time goes:
time: 407 us; the launch traced here: 404 us
  waiting for transfers between devices  210 us (52%)
  other arithmetic  115 us (28%)
  starting transfers between devices  61.1 us (15%)
  local copies, waits for them, and re-layouts  16.8 us (4%)
    ppermute x12, waiting for transfers between devices, extended(): before = lax.ppermute(last, axis, up)  177 us
    add x4, other arithmetic, march_step(): return 2.0 * middle - before + speed_square * spread  114 us
    ppermute x12, starting transfers between devices, extended(): before = lax.ppermute(last, axis, up)  45.6 us
    ppermute x12, waiting for transfers between devices, extended(): after = lax.ppermute(initial, axis, down)  32.9 us
    ppermute x12, starting transfers between devices, extended(): after = lax.ppermute(initial, axis, down)  15.5 us
  transfers between devices with their start and end apart: 24, of which 20 were waited for; matrix products, arithmetic and copies ran while one was open for 1% of the time, Pallas kernels for 0%

commit v1 on v0

v1 whole, which is shorter than its diff:
```python
import functools

import jax
import jax.numpy as jnp
from jax import lax
from jax.experimental import pallas as pl
from jax.experimental.pallas import tpu as pltpu
from jax.sharding import PartitionSpec as P

STEPS = 4
ROWS = 8
AXES = ("lat", "lon", "lev")


def kernel(peers, field, earlier, speed, out, even, odd, squares, lat_halo, lev_halo, lev_edge,
           lat_sent, lat_come, lon_sent, lon_come, lev_sent, lev_come, loaded, stored):
    J, I, K, M = field.shape
    rows = ROWS if I % ROWS == 0 else 1
    chunks = I // rows
    bufs = (even, odd)
    at = {axis: lax.axis_index(axis) for axis in AXES}
    has = {axis: (at[axis] > 0, at[axis] < peers[axis] - 1) for axis in AXES}
    ids = {axis: (lax.rem(at[axis] + peers[axis] - 1, peers[axis]), lax.rem(at[axis] + 1, peers[axis])) for axis in AXES}

    def remote(axis, side, src, dst, sent, come):
        return pltpu.make_async_remote_copy(
            src_ref=src, dst_ref=dst, send_sem=sent, recv_sem=come,
            device_id={axis: ids[axis][side]}, device_id_type=pl.DeviceIdType.MESH)

    def lat_copy(step, side, c):
        j = (J - 1) * side
        here = pl.ds(c * rows, rows)
        src = field.at[j, here] if step == 0 else bufs[step % 2].at[j, pl.ds(c * rows + 1, rows)]
        return remote("lat", side, src, lat_halo.at[step, 1 - side, here],
                      lat_sent.at[step, side, c], lat_come.at[step, 1 - side, c])

    def lon_copy(step, side):
        src = field.at[:, (I - 1) * side] if step == 0 else bufs[step % 2].at[:, 1 + (I - 1) * side]
        return remote("lon", side, src, bufs[step % 2].at[:, (I + 1) * (1 - side)],
                      lon_sent.at[step, side], lon_come.at[step, 1 - side])

    def lev_copy(step, side):
        return remote("lev", side, lev_edge.at[step, side], lev_halo.at[step, 1 - side],
                      lev_sent.at[step, side], lev_come.at[step, 1 - side])

    def each_side(axis, act):
        for side in (0, 1):
            pl.when(has[axis][side])(functools.partial(act, side))

    def load(which, c):
        src, dst, first = ((field, even, 1), (earlier, odd, 1), (speed, squares, 0))[which]
        return pltpu.make_async_copy(src.at[:, pl.ds(c * rows, rows)],
                                     dst.at[:, pl.ds(c * rows + first, rows)], loaded.at[which, c])

    def store(c):
        return pltpu.make_async_copy(bufs[STEPS % 2].at[:, pl.ds(c * rows + 1, rows)],
                                     out.at[:, pl.ds(c * rows, rows)], stored.at[c])

    def loop(count, body):
        lax.fori_loop(0, count, lambda n, carry: (body(n), carry)[1], 0)

    barrier = pltpu.get_barrier_semaphore()
    for axis in AXES:
        each_side(axis, lambda side: pl.semaphore_signal(
            barrier, inc=1, device_id={axis: ids[axis][side]}, device_id_type=pl.DeviceIdType.MESH))
    for which in range(3):
        loop(chunks, lambda c: load(which, c).start())
    pl.semaphore_wait(barrier, sum(there.astype(jnp.int32) for axis in AXES for there in has[axis]))

    @functools.partial(loop, chunks)
    def _(c):
        each_side("lat", lambda side: lat_copy(0, side, c).start())

    each_side("lon", lambda side: lon_copy(0, side).start())

    for side in (0, 1):
        @pl.when(jnp.logical_not(has["lat"][side]))
        def _():
            @functools.partial(loop, I)
            def _(i):
                for step in range(STEPS):
                    lat_halo[step, side, i] = jnp.zeros((K, M), jnp.float32)

        @pl.when(jnp.logical_not(has["lon"][side]))
        def _():
            for buf in bufs:
                for j in range(J):
                    buf[j, (I + 1) * side] = jnp.zeros((K, M), jnp.float32)

        @pl.when(jnp.logical_not(has["lev"][side]))
        def _():
            for step in range(STEPS):
                for j in range(J):
                    lev_halo[step, side, j] = jnp.zeros((I, M), jnp.float32)

    loop(chunks, lambda c: load(0, c).wait())

    @functools.partial(loop, I)
    def _(i):
        for j in range(J):
            for side in (0, 1):
                lev_edge[0, side, j, pl.ds(i, 1), :] = even[j, i + 1, pl.ds((K - 1) * side, 1), :]

    each_side("lev", lambda side: lev_copy(0, side).start())

    level = lax.broadcasted_iota(jnp.int32, (K, M), 0)
    for step in range(STEPS):
        now, then = bufs[step % 2], bufs[(step + 1) % 2]

        def row(i):
            for j in range(J):
                middle = now[j, i + 1]
                below = lat_halo[step, 0, i] if j == 0 else now[j - 1, i + 1]
                above = lat_halo[step, 1, i] if j == J - 1 else now[j + 1, i + 1]
                under = jnp.where(level == 0, lev_halo[step, 0, j, pl.ds(i, 1), :], pltpu.roll(middle, 1, 0))
                over = jnp.where(level == K - 1, lev_halo[step, 1, j, pl.ds(i, 1), :], pltpu.roll(middle, K - 1, 0))
                spread = below + above + now[j, i] + now[j, i + 2] + under + over - 6.0 * middle
                later = 2.0 * middle - then[j, i + 1] + squares[j, i] * spread
                then[j, i + 1] = later
                if step + 1 < STEPS:
                    lev_edge[step + 1, 0, j, pl.ds(i, 1), :] = later[:1]
                    lev_edge[step + 1, 1, j, pl.ds(i, 1), :] = later[K - 1:]

        for axis, copy in (("lon", lon_copy), ("lev", lev_copy)):
            if step > 0:
                each_side(axis, lambda side: copy(step - 1, side).wait_send())
            each_side(axis, lambda side: copy(step, 1 - side).wait_recv())

        @functools.partial(loop, chunks)
        def _(c):
            if step == 0:
                load(1, c).wait()
                load(2, c).wait()
            else:
                each_side("lat", lambda side: lat_copy(step - 1, side, c).wait_send())
            each_side("lat", lambda side: lat_copy(step, 1 - side, c).wait_recv())
            loop(rows, lambda r: row(c * rows + r))
            if step + 1 < STEPS:
                each_side("lat", lambda side: lat_copy(step + 1, side, c).start())
            else:
                store(c).start()

        if step + 1 < STEPS:
            each_side("lon", lambda side: lon_copy(step + 1, side).start())
            each_side("lev", lambda side: lev_copy(step + 1, side).start())

    for axis, copy in (("lon", lon_copy), ("lev", lev_copy)):
        each_side(axis, lambda side: copy(STEPS - 1, side).wait_send())

    @functools.partial(loop, chunks)
    def _(c):
        each_side("lat", lambda side: lat_copy(STEPS - 1, side, c).wait_send())
        store(c).wait()


def solution(mesh):
    peers = {axis: mesh.shape[axis] for axis in AXES}

    def local(field_now, earlier, speed_square):
        J, I, K, M = field_now.shape
        chunks = I // ROWS if I % ROWS == 0 else I
        dma = pltpu.SemaphoreType.DMA
        return pl.pallas_call(
            functools.partial(kernel, peers),
            out_shape=jax.ShapeDtypeStruct(field_now.shape, jnp.float32),
            in_specs=[pl.BlockSpec(memory_space=pltpu.HBM)] * 3,
            out_specs=pl.BlockSpec(memory_space=pltpu.HBM),
            scratch_shapes=[
                pltpu.VMEM((J, I + 2, K, M), jnp.float32),
                pltpu.VMEM((J, I + 2, K, M), jnp.float32),
                pltpu.VMEM((J, I, K, M), jnp.float32),
                pltpu.VMEM((STEPS, 2, I, K, M), jnp.float32),
                pltpu.VMEM((STEPS, 2, J, I, M), jnp.float32),
                pltpu.VMEM((STEPS, 2, J, I, M), jnp.float32),
                dma((STEPS, 2, chunks)), dma((STEPS, 2, chunks)),
                dma((STEPS, 2)), dma((STEPS, 2)),
                dma((STEPS, 2)), dma((STEPS, 2)),
                dma((3, chunks)), dma((chunks,)),
            ],
            compiler_params=pltpu.CompilerParams(
                collective_id=0, has_side_effects=True, vmem_limit_bytes=60 * 1024 * 1024),
        )(field_now, earlier, speed_square)

    spec = P("lat", "lon", "lev", None)
    return jax.shard_map(local, mesh=mesh, in_specs=(spec, spec, spec), out_specs=spec, check_vma=False)
```

time: 407 us -> 197 us (0.48)
  waiting for transfers between devices: 210 us -> 0 us
  Pallas kernels: 0 us -> 189 us
  other arithmetic: 115 us -> 0 us
  starting transfers between devices: 61.1 us -> 0 us
  local copies, waits for them, and re-layouts: 16.8 us -> 8.44 us
    ppermute x24 -> x0, waiting for transfers between devices: 210 us -> none  [the longest x12 177 us: extended(): before = lax.ppermute(last, axis, up)]
    pallas_call x0 -> x1, Pallas kernels: none -> 189 us  [local(): pl.pallas_call(functools.partial(kernel, peers), out_shape=jax.ShapeDtype...]
    add x4 -> x0, other arithmetic: 114 us -> none  [march_step(): return 2.0 * middle - before + speed_square * spread]
    ppermute x24 -> x0, starting transfers between devices: 61.1 us -> none  [the longest x12 45.6 us: extended(): before = lax.ppermute(last, axis, up)]
    slice x13 -> x0, local copies, waits for them, and re-layouts: 10.2 us -> none  [the longest x8 6 us: extended(): last = lax.slice_in_dim(value, length - width, length, axis=dim)]
    unnamed x20 -> x1, local copies, waits for them, and re-layouts: 3.22 us -> 8.44 us
  transfers between devices with their start and end apart: 24 -> 0, of which waited for: 20 -> 0; matrix products, arithmetic and copies ran while one was open for 1% -> 0% of each run, Pallas kernels for 0% -> 0%
where the time goes in v1:
time: 197 us
  Pallas kernels  189 us (96%)
  local copies, waits for them, and re-layouts  8.44 us (4%)
    pallas_call x1, Pallas kernels, local(): pl.pallas_call(functools.partial(kernel, peers), out_shape=jax.ShapeDtype...  189 us
    unnamed x1, local copies, waits for them, and re-layouts  8.44 us

profile of v1, /device:TPU:0, one launch (start us, length us, event | category | flops | bytes accessed | tf_op | source)
XLA Modules:
  0.0 197.2 jit_solution(3584565817156403615)
XLA Ops:
  0.0 188.8 %shard_map.37 = f32[4,64,64,128]{3,2,1,0:T(8,128)} custom-call(f32[4,64,64,128]{3,2,1,0:T(8,128)} %field.1, f32[4,64,64,128]{3,2,1,0:T(8,128)} %earlier.1, f32[4,64,64,128]{3,2,1,0:T(8,128)} %speed.1), custom_call_target="tpu_custom_call" | custom-call | tf_op jit(solution)/shard_map/pallas_call | solution.py:163
  188.8 8.4 %copy.5 = f32[4,64,64,128]{3,2,1,0:T(8,128)} copy(f32[4,64,64,128]{3,2,1,0:T(8,128)} %shard_map.37) | data formatting | bytes 16777216

commit v2 on v1

--- a/solution.py
+++ b/solution.py
@@ -8,15 +8,21 @@
 from jax.sharding import PartitionSpec as P
 
 STEPS = 4
-ROWS = 8
 AXES = ("lat", "lon", "lev")
 
 
+def pieces(I):
+    unit = I // 16
+    table = [[4, 4, 4, 4]] * (STEPS - 1) + [[4, 4, 4, 2, 1, 1]]
+    if I % 16:
+        unit, table = I, [[1]] * STEPS
+    return [[(unit * sum(sizes[:n]), unit * size) for n, size in enumerate(sizes)] for sizes in table]
+
+
 def kernel(peers, field, earlier, speed, out, even, odd, squares, lat_halo, lev_halo, lev_edge,
-           lat_sent, lat_come, lon_sent, lon_come, lev_sent, lev_come, loaded, stored):
+           lat_sent, lat_come, lon_sent, lon_come, lev_sent, lev_come, loaded):
     J, I, K, M = field.shape
-    rows = ROWS if I % ROWS == 0 else 1
-    chunks = I // rows
+    parts = pieces(I)
     bufs = (even, odd)
     at = {axis: lax.axis_index(axis) for axis in AXES}
     has = {axis: (at[axis] > 0, at[axis] < peers[axis] - 1) for axis in AXES}
@@ -29,8 +35,9 @@
 
     def lat_copy(step, side, c):
         j = (J - 1) * side
-        here = pl.ds(c * rows, rows)
-        src = field.at[j, here] if step == 0 else bufs[step % 2].at[j, pl.ds(c * rows + 1, rows)]
+        first, rows = parts[step][c]
+        here = pl.ds(first, rows)
+        src = field.at[j, here] if step == 0 else bufs[step % 2].at[j, pl.ds(first + 1, rows)]
         return remote("lat", side, src, lat_halo.at[step, 1 - side, here],
                       lat_sent.at[step, side, c], lat_come.at[step, 1 - side, c])
 
@@ -48,13 +55,10 @@
             pl.when(has[axis][side])(functools.partial(act, side))
 
     def load(which, c):
-        src, dst, first = ((field, even, 1), (earlier, odd, 1), (speed, squares, 0))[which]
-        return pltpu.make_async_copy(src.at[:, pl.ds(c * rows, rows)],
-                                     dst.at[:, pl.ds(c * rows + first, rows)], loaded.at[which, c])
-
-    def store(c):
-        return pltpu.make_async_copy(bufs[STEPS % 2].at[:, pl.ds(c * rows + 1, rows)],
-                                     out.at[:, pl.ds(c * rows, rows)], stored.at[c])
+        src, dst, margin = ((field, even, 1), (earlier, odd, 1), (speed, squares, 0))[which]
+        first, rows = parts[0][c]
+        return pltpu.make_async_copy(src.at[:, pl.ds(first, rows)],
+                                     dst.at[:, pl.ds(first + margin, rows)], loaded.at[which, c])
 
     def loop(count, body):
         lax.fori_loop(0, count, lambda n, carry: (body(n), carry)[1], 0)
@@ -64,11 +68,11 @@
         each_side(axis, lambda side: pl.semaphore_signal(
             barrier, inc=1, device_id={axis: ids[axis][side]}, device_id_type=pl.DeviceIdType.MESH))
     for which in range(3):
-        loop(chunks, lambda c: load(which, c).start())
+        for c in range(len(parts[0])):
+            load(which, c).start()
     pl.semaphore_wait(barrier, sum(there.astype(jnp.int32) for axis in AXES for there in has[axis]))
 
-    @functools.partial(loop, chunks)
-    def _(c):
+    for c in range(len(parts[0])):
         each_side("lat", lambda side: lat_copy(0, side, c).start())
 
     each_side("lon", lambda side: lon_copy(0, side).start())
@@ -93,7 +97,8 @@
                 for j in range(J):
                     lev_halo[step, side, j] = jnp.zeros((I, M), jnp.float32)
 
-    loop(chunks, lambda c: load(0, c).wait())
+    for c in range(len(parts[0])):
+        load(0, c).wait()
 
     @functools.partial(loop, I)
     def _(i):
@@ -107,8 +112,8 @@
     for step in range(STEPS):
         now, then = bufs[step % 2], bufs[(step + 1) % 2]
 
-        def row(i):
-            for j in range(J):
+        def row(i, planes):
+            for j in planes:
                 middle = now[j, i + 1]
                 below = lat_halo[step, 0, i] if j == 0 else now[j - 1, i + 1]
                 above = lat_halo[step, 1, i] if j == J - 1 else now[j + 1, i + 1]
@@ -116,8 +121,10 @@
                 over = jnp.where(level == K - 1, lev_halo[step, 1, j, pl.ds(i, 1), :], pltpu.roll(middle, K - 1, 0))
                 spread = below + above + now[j, i] + now[j, i + 2] + under + over - 6.0 * middle
                 later = 2.0 * middle - then[j, i + 1] + squares[j, i] * spread
-                then[j, i + 1] = later
-                if step + 1 < STEPS:
+                if step + 1 == STEPS:
+                    out[j, i] = later
+                else:
+                    then[j, i + 1] = later
                     lev_edge[step + 1, 0, j, pl.ds(i, 1), :] = later[:1]
                     lev_edge[step + 1, 1, j, pl.ds(i, 1), :] = later[K - 1:]
 
@@ -126,19 +133,23 @@
                 each_side(axis, lambda side: copy(step - 1, side).wait_send())
             each_side(axis, lambda side: copy(step, 1 - side).wait_recv())
 
-        @functools.partial(loop, chunks)
-        def _(c):
+        if step + 1 == STEPS:
+            for c in range(len(parts[step - 1])):
+                each_side("lat", lambda side: lat_copy(step - 1, side, c).wait_send())
+            loop(I, lambda i: row(i, range(1, J - 1)))
+        for c, (first, rows) in enumerate(parts[step]):
             if step == 0:
                 load(1, c).wait()
                 load(2, c).wait()
-            else:
+            elif step + 1 < STEPS:
                 each_side("lat", lambda side: lat_copy(step - 1, side, c).wait_send())
             each_side("lat", lambda side: lat_copy(step, 1 - side, c).wait_recv())
-            loop(rows, lambda r: row(c * rows + r))
+            planes = (0, J - 1)[: min(J, 2)] if step + 1 == STEPS else range(J)
+            loop(rows, lambda r: row(first + r, planes))
             if step + 1 < STEPS:
-                each_side("lat", lambda side: lat_copy(step + 1, side, c).start())
-            else:
-                store(c).start()
+                for d, (start, size) in enumerate(parts[step + 1]):
+                    if first < start + size <= first + rows:
+                        each_side("lat", lambda side: lat_copy(step + 1, side, d).start())
 
         if step + 1 < STEPS:
             each_side("lon", lambda side: lon_copy(step + 1, side).start())
@@ -147,10 +158,8 @@
     for axis, copy in (("lon", lon_copy), ("lev", lev_copy)):
         each_side(axis, lambda side: copy(STEPS - 1, side).wait_send())
 
-    @functools.partial(loop, chunks)
-    def _(c):
+    for c in range(len(parts[-1])):
         each_side("lat", lambda side: lat_copy(STEPS - 1, side, c).wait_send())
-        store(c).wait()
 
 
 def solution(mesh):
@@ -158,13 +167,13 @@
 
     def local(field_now, earlier, speed_square):
         J, I, K, M = field_now.shape
-        chunks = I // ROWS if I % ROWS == 0 else I
+        chunks = max(len(part) for part in pieces(I))
         dma = pltpu.SemaphoreType.DMA
         return pl.pallas_call(
             functools.partial(kernel, peers),
-            out_shape=jax.ShapeDtypeStruct(field_now.shape, jnp.float32),
+            out_shape=pltpu.VMEM(field_now.shape, jnp.float32),
             in_specs=[pl.BlockSpec(memory_space=pltpu.HBM)] * 3,
-            out_specs=pl.BlockSpec(memory_space=pltpu.HBM),
+            out_specs=pl.BlockSpec(memory_space=pltpu.VMEM),
             scratch_shapes=[
                 pltpu.VMEM((J, I + 2, K, M), jnp.float32),
                 pltpu.VMEM((J, I + 2, K, M), jnp.float32),
@@ -175,10 +184,10 @@
                 dma((STEPS, 2, chunks)), dma((STEPS, 2, chunks)),
                 dma((STEPS, 2)), dma((STEPS, 2)),
                 dma((STEPS, 2)), dma((STEPS, 2)),
-                dma((3, chunks)), dma((chunks,)),
+                dma((3, chunks)),
             ],
             compiler_params=pltpu.CompilerParams(
-                collective_id=0, has_side_effects=True, vmem_limit_bytes=60 * 1024 * 1024),
+                collective_id=0, has_side_effects=True, vmem_limit_bytes=48000 * 1024),
         )(field_now, earlier, speed_square)
 
     spec = P("lat", "lon", "lev", None)

time: 197 us -> 191 us (0.970)
  local copies, waits for them, and re-layouts: 8.44 us -> 3.4 us
  Pallas kernels: 189 us -> 187 us
    unnamed x1, local copies, waits for them, and re-layouts: 8.44 us -> 3.4 us
where the time goes in v2:
time: 191 us; the launch traced here: 190 us
  Pallas kernels  187 us (98%)
  local copies, waits for them, and re-layouts  3.4 us (2%)
    pallas_call x1, Pallas kernels, local(): pl.pallas_call(functools.partial(kernel, peers), out_shape=pltpu.VMEM(fie...  187 us

profile of v2, /device:TPU:0, one launch (start us, length us, event | category | flops | bytes accessed | tf_op | source)
XLA Modules:
  0.0 190.4 jit_solution(6356299452570195345)
XLA Ops:
  0.0 187.0 %shard_map.37 = f32[4,64,64,128]{3,2,1,0:T(8,128)S(1)} custom-call(f32[4,64,64,128]{3,2,1,0:T(8,128)} %field.1, f32[4,64,64,128]{3,2,1,0:T(8,128)} %earlier.1, f32[4,64,64,128]{3,2,1,0:T(8,128)} %speed.1), custom_call_target="tpu_custom_call" | custom-call | tf_op jit(solution)/shard_map/pallas_call | solution.py:172
  187.0 3.4 %copy.5 = f32[4,64,64,128]{3,2,1,0:T(8,128)} copy(f32[4,64,64,128]{3,2,1,0:T(8,128)S(1)} %shard_map.37) | data formatting | bytes 16777216

commit v3 on v2

--- a/solution.py
+++ b/solution.py
@@ -13,7 +13,7 @@
 
 def pieces(I):
     unit = I // 16
-    table = [[4, 4, 4, 4]] * (STEPS - 1) + [[4, 4, 4, 2, 1, 1]]
+    table = [[8, 4, 4]] * (STEPS - 1) + [[8, 4, 2, 2]]
     if I % 16:
         unit, table = I, [[1]] * STEPS
     return [[(unit * sum(sizes[:n]), unit * size) for n, size in enumerate(sizes)] for sizes in table]

time: 191 us -> 190 us (level)
  no operation moved by 1% of the time
where the time goes in v3:
time: 190 us
  Pallas kernels  187 us (98%)
  local copies, waits for them, and re-layouts  3.4 us (2%)
    pallas_call x1, Pallas kernels, local(): pl.pallas_call(functools.partial(kernel, peers), out_shape=pltpu.VMEM(fie...  187 us

profile of v3, /device:TPU:0, one launch (start us, length us, event | category | flops | bytes accessed | tf_op | source)
XLA Modules:
  0.0 190.2 jit_solution(11622601317253942727)
XLA Ops:
  0.0 186.8 %shard_map.37 = f32[4,64,64,128]{3,2,1,0:T(8,128)S(1)} custom-call(f32[4,64,64,128]{3,2,1,0:T(8,128)} %field.1, f32[4,64,64,128]{3,2,1,0:T(8,128)} %earlier.1, f32[4,64,64,128]{3,2,1,0:T(8,128)} %speed.1), custom_call_target="tpu_custom_call" | custom-call | tf_op jit(solution)/shard_map/pallas_call | solution.py:172
  186.8 3.4 %copy.5 = f32[4,64,64,128]{3,2,1,0:T(8,128)} copy(f32[4,64,64,128]{3,2,1,0:T(8,128)S(1)} %shard_map.37) | data formatting | bytes 16777216
